TPU v7x, 32 devices: a whole 2x2x4 slice. The times are simulated.
32 devices in a mesh: dp: 4 (over y, x), cls: 8 (over z, core).
Axes of the slice: x: 2, y: 2, z: 4, core: 2. Of those that a mesh axis runs over, the one named last changes fastest.
Arguments:
- sketches: bfloat16 [8192, 4096], P(('dp', 'cls')), may hold values from -6 to 6
- labels: int32 [8192], P(('dp', 'cls')), may hold values from 0 to 7, as said below
- places: int32 [8192], P(('dp', 'cls')), may hold values from 0 to 2047, as said below
- counts: int32 [8, 4, 32], P('cls'), may hold values from 0 to 16, as said below
- chosen: int32 [3, 8], P(None, 'cls'), may hold values from 0 to 2047, as said below
Outputs:
- gain_scores: float32 [3, 8, 2048], P(None, 'cls', 'dp')
- coverage: float32 [8, 2048], P('cls', 'dp')
Inputs may be any that keep to these rules, and one draw needn't show every extreme that they name: `labels`: every class has 4 or more examples. `places`: an example of device s (its index along dp and cls together) with class k has place m * 512 + s * 16 + j in class k's block: m is the member of dp that receives it, and for each k, m and s the j run over 0 to counts[k, m, s] - 1 without gaps, so no two examples share a place. In every draw one class and member receive 16 examples from every device. counts[k, m, s] is the number of examples of device s that take places of class k on member m. chosen[t, k] is a place of class k's block that holds an example; the 3 picks of a class differ.
All inputs are finite; a program needn't handle non-finite values.
Results may differ from a plain program's by a relative error of at most 0.0003.
Values may be sent and summed in bfloat16 or wider, within the bound.
A program may use at most 128 MiB of HBM per device.

v0:
```python
import jax
import jax.numpy as jnp
from jax import lax
from jax.sharding import PartitionSpec as P


def squared_norms(matrix):
    wide = matrix.astype(jnp.float32)
    return jnp.sum(wide * wide, axis=1)


def distances(left, left_norms, right, right_norms, width):
    inner = lax.dot_general(
        left, right, (((1,), (1,)), ((), ())), preferred_element_type=jnp.float32
    )
    return (left_norms[:, None] + right_norms[None, :] - 2.0 * inner) / width


def coverage_chain(similar_picks):
    current = jnp.zeros((similar_picks.shape[0],), jnp.float32)
    before = []
    for turn_index in range(similar_picks.shape[1]):
        before.append(current)
        current = jnp.maximum(current, similar_picks[:, turn_index])
    return (jnp.stack(before, axis=1), current)


def column_gains(similar, row_weight, row_cover):
    return jnp.stack(
        [
            jnp.sum(
                row_weight[:, None] * jnp.maximum(similar - row_cover[:, turn_index][:, None], 0.0),
                axis=0,
            )
            for turn_index in range(row_cover.shape[1])
        ]
    )


def masked_largest(pair_block, row_weight, column_weight):
    return jnp.max(jnp.where(row_weight[:, None] * column_weight[None, :] > 0.0, pair_block, 0.0))


def body(sketches, labels, places, counts, chosen):
    row_count, width = sketches.shape
    members = lax.axis_size("dp")
    owners = lax.axis_size("cls")
    devices = members * owners
    per_source = 2 * row_count // devices
    capacity = devices * per_source
    member = lax.axis_index("dp")
    picked = chosen[:, 0]
    pick_count = picked.shape[0]
    target = (places // capacity * owners + labels) * per_source + places % per_source
    send_table = (
        lax.broadcasted_iota(jnp.int32, (2 * row_count, row_count), 0) == target[None, :]
    ).astype(jnp.bfloat16)
    outgoing = jnp.dot(send_table, sketches, preferred_element_type=jnp.float32).astype(
        jnp.bfloat16
    )
    arrived = lax.all_to_all(
        outgoing.reshape(devices, per_source, width),
        ("dp", "cls"),
        split_axis=0,
        concat_axis=0,
        tiled=True,
    )
    local_rows = arrived.reshape(capacity, width)
    class_counts = counts[0]
    valid_all = (
        (
            lax.broadcasted_iota(jnp.int32, (members, devices, per_source), 2)
            < class_counts[:, :, None]
        )
        .reshape(members, capacity)
        .astype(jnp.float32)
    )
    own_valid = lax.dynamic_index_in_dim(valid_all, member, 0, keepdims=False)
    total = jnp.sum(class_counts).astype(jnp.float32)
    local_norms = squared_norms(local_rows)
    block_rows = lax.all_gather(local_rows, "dp", axis=0, tiled=True)
    spread_all = distances(local_rows, local_norms, block_rows, squared_norms(block_rows), width)
    largest = masked_largest(spread_all, own_valid, valid_all.reshape(-1))
    bound = lax.pmax(largest, "dp")
    similar = bound - spread_all
    pick_columns = jnp.stack(
        [
            lax.dynamic_index_in_dim(similar, picked[turn_index], 1, keepdims=False)
            for turn_index in range(pick_count)
        ],
        axis=1,
    )
    cover_before, cover_final = coverage_chain(pick_columns)
    partial_value = column_gains(similar, own_valid, cover_before)
    summed = lax.psum_scatter(partial_value, "dp", scatter_dimension=1, tiled=True)
    gain_scores = (summed * own_valid[None, :] / total)[:, None, :]
    coverage = (cover_final * own_valid)[None, :]
    return (gain_scores, coverage)


def solution(mesh):
    placed = (
        P(("dp", "cls"), None),
        P(("dp", "cls")),
        P(("dp", "cls")),
        P("cls", None, None),
        P(None, "cls"),
    )
    return jax.shard_map(
        body,
        mesh=mesh,
        in_specs=placed,
        out_specs=(P(None, "cls", "dp"), P("cls", "dp")),
        check_vma=False,
    )
```

profile of v0, /device:TPU:8, one launch (start us, length us, event | category | flops | bytes accessed | tf_op | source)
XLA Modules:
  0.0 344.0 jit_solution(5986665020322543022)
XLA Ops:
  7.2 0.8 fusion.3
  8.1 0.7 copy-done
  8.8 1.3 convolution_convert_fusion
  10.1 98.0 %all_to_all.5 = bf16[32,16,4096]{2,1,0:T(8,128)(2,1)} all-to-all(bf16[32,16,4096]{2,1,0:T(8,128)(2,1)S(1)} %bitcast.23), channel_id=1, replica_groups=mesh['dp'=4,'cls'=8] {'dp','cls'}, dimensions={0} | all-to-all | bytes 8388608 | tf_op jit(solution)/shard_map/all_to_all | solution.py:61
  108.1 0.6 copy-done.3
  108.8 0.1 lt.43
  108.9 0.1 lt.46
  109.0 0.6 fusion.4
  113.4 0.1 iota.25
  115.5 4.2 %multiply_reduce_fusion.1 = f32[32,16]{1,0:T(8,128)S(1)} fusion(bf16[32,16,4096]{2,1,0:T(8,128)(2,1)} %all_to_all.5), kind=kLoop, calls=%fused_computation.1 | loop fusion | flops 6290944 | bytes 4196352 | tf_op jit(solution)/shard_map/reduce_sum | solution.py:9
  119.7 0.1 add.48
  119.7 146.1 %all-gather.2.cloned.1.call-done = bf16[2048,4096]{1,0:T(8,128)(2,1)} async-done(((bf16[512,4096]{1,0:T(8,128)(2,1)}), bf16[2048,4096]{1,0:T(8,128)(2,1)}) %all-gather.2.cloned.1.call-update) | async-done | bytes 16777232 | tf_op jit(solution)/shard_map/all_gather | solution.py:81
  265.8 7.5 %multiply_reduce_fusion = f32[2048]{0:T(1024)S(1)} fusion(bf16[2048,4096]{1,0:T(8,128)(2,1)} %all-gather.2.cloned.1.call-done), kind=kLoop, calls=%fused_computation | loop fusion | flops 25163776 | bytes 16785408 | tf_op jit(solution)/shard_map/reduce_sum | solution.py:9
  273.3 15.0 %select_reduce_fusion = (f32[]{:T(128)}, f32[512,2048]{1,0:T(8,128)}) fusion(f32[2048]{0:T(1024)S(1)} %compare_convert_fusion, f32[512]{0:T(512)S(1)} %bitcast.29, bf16[512,4096]{1,0:T(8,128)(2,1)S(1)} %bitcast.22, bf16[2048,4096]{1,0:T(8,128)(2,1)} %all-gather.2.cloned.1.call-done, f32[2048]{0:T(1024)S(1)} %multiply_reduce_fusion, f32[512]{0:T(512)S(1)} %add.48), kind=kOutput, calls=%fused_computation.6 | convolution fusion | flops 8598323200 | bytes 25186308 | tf_op jit(solution)/shard_map/dot_general | solution.py:13
  288.4 9.5 %pmax.7 = f32[]{:T(128)} all-reduce(f32[]{:T(128)} %get-tuple-element.13), channel_id=1, replica_groups=mesh['dp'=4,'cls'=8] {'dp'}, use_global_device_ids=true, to_apply=%region_3.4 | all-reduce | flops 1 | bytes 8 | tf_op jit(solution)/shard_map/pmax | solution.py:84
  297.9 3.4 %broadcast_subtract_fusion = f32[512,2048]{1,0:T(8,128)S(1)} fusion(f32[512,2048]{1,0:T(8,128)} %get-tuple-element.14, f32[]{:T(128)} %pmax.7), kind=kLoop, calls=%fused_computation.9 | loop fusion | flops 1048576 | bytes 8388612 | tf_op jit(solution)/shard_map/sub | solution.py:85
  301.3 0.5 maximum_reduce_fusion
  301.9 4.1 %multiply_reduce_fusion.4 = (f32[2048]{0:T(1024)S(1)}, f32[2048]{0:T(1024)S(1)}, f32[2048]{0:T(1024)S(1)}) fusion(f32[512]{0:T(512)S(1)} %bitcast.30, f32[512]{0:T(512)S(1)} %get-tuple-element.8, f32[512]{0:T(512)S(1)} %get-tuple-element.9, f32[512,2048]{1,0:T(8,128)S(1)} %copy-done.2, f32[]{:T(128)} %pmax.7), kind=kLoop, calls=%fused_computation.5 | loop fusion | flops 12576768 | bytes 4225028 | tf_op jit(solution)/shard_map/reduce_sum | solution.py:31
  306.0 1.4 copy.8
  307.4 0.6 reduce_sum.59
  308.7 0.6 mul.87
  309.3 26.2 %reduce-scatter.4.cloned.1.call-done = f32[512,3]{1,0:T(8,128)} async-done(((f32[2048,3]{1,0:T(8,128)}), f32[512,3]{1,0:T(8,128)}) %reduce-scatter.4.cloned.1.call-update) | async-done | bytes 6160
  335.5 1.1 copy.9
  336.6 0.6 copy.7
  (20 shorter events, 0.3 us)
Async XLA Ops:
  7.2 1.6 copy-start
  7.2 258.7 %all-gather.2.cloned.1.call-start = ((), (), s32[]{:S(2)}) async-start(), calls=%async_computation.2 | async-start | bytes 20971520 | tf_op jit(solution)/shard_map/all_gather | solution.py:81
  108.1 0.7 copy-start.3
  108.1 0.9 copy-start.4
  108.1 227.4 %reduce-scatter.4.cloned.1.call-start = ((), (), s32[]{:S(2)}) async-start(), calls=%async_computation.3 | async-start | bytes 1310720
  265.8 7.5 %copy-start.1 = (bf16[32,16,4096]{2,1,0:T(8,128)(2,1)S(1)}, bf16[32,16,4096]{2,1,0:T(8,128)(2,1)}, u32[]{:S(2)}) copy-start(bf16[32,16,4096]{2,1,0:T(8,128)(2,1)} %all_to_all.5) | copy-start | bytes 12582916
  297.9 4.0 %copy-start.2 = (f32[512,2048]{1,0:T(8,128)S(1)}, f32[512,2048]{1,0:T(8,128)}, u32[]{:S(2)}) copy-start(f32[512,2048]{1,0:T(8,128)} %get-tuple-element.14) | copy-start | bytes 12582916
Sparse Core Ops, SparseCore 0:
  108.2 157.5 all-gather.1
  307.5 27.9 reduce-scatter.3
where the time goes:
time: 346 us; the launch traced here: 344 us
  waiting for transfers between devices  172 us (50%)
  blocking collectives  108 us (31%)
  other arithmetic  21.9 us (6%)
  between operations  20.5 us (6%)
  matrix products  16.3 us (5%)
  local copies, waits for them, and re-layouts  5.43 us (2%)
    all_gather x1, waiting for transfers between devices, body(): block_rows = lax.all_gather(local_rows, 'dp', axis=0, tiled=True)  146 us
    all_to_all x1, blocking collectives, body(): lax.all_to_all(outgoing.reshape(devices, per_source, width), ('dp', 'cls'...  98 us
    unnamed x3, waiting for transfers between devices  26.2 us
    dot_general x1, matrix products, distances(): lax.dot_general(left, right, (((1,), (1,)), ((), ())), preferred_element_...  15 us
    reduce_sum x2, other arithmetic, squared_norms(): return jnp.sum(wide * wide, axis=1)  11.7 us
    pmax x1, blocking collectives, body(): bound = lax.pmax(largest, 'dp')  9.54 us
  transfers between devices with their start and end apart: 2, of which 2 were waited for; matrix products, arithmetic and copies ran while one was open for 2% of the time, Pallas kernels for 0%

commit v1 on v0

v1 whole, which is shorter than its diff:
```python
import functools

import jax
import jax.numpy as jnp
from jax import lax
from jax.experimental import pallas as pl
from jax.experimental.pallas import tpu as pltpu
from jax.sharding import PartitionSpec as P

MESH = pl.DeviceIdType.MESH


def ring_place(index):
    high = index // 2
    return 2 * high + (index % 2 + high) % 2


def ring_member(place):
    high = place // 2
    return 2 * high + (place % 2 + high) % 2


def exchange_kernel(members, owners, out_ref, rows_ref, a_send, a_recv, own_sem, b_send, b_recv):
    member = lax.axis_index("dp")
    owner = lax.axis_index("cls")
    half = members // 2
    place = ring_place(member)
    side = owner % 2
    step = 1 - 2 * side

    barrier = pltpu.get_barrier_semaphore()
    for hop in range(1, owners):
        pl.semaphore_signal(
            barrier, inc=1, device_id=(member, (owner + hop) % owners), device_id_type=MESH
        )
    for hop in range(1, members):
        pl.semaphore_signal(
            barrier,
            inc=1,
            device_id=(ring_member((place + hop) % members), owner),
            device_id_type=MESH,
        )
    pl.semaphore_wait(barrier, owners + members - 2)

    def dispatch(chunk, hop):
        target = (owner + hop) % owners
        return pltpu.make_async_remote_copy(
            src_ref=out_ref.at[target, chunk],
            dst_ref=rows_ref.at[0, chunk, owner],
            send_sem=a_send.at[chunk, hop - 1],
            recv_sem=a_recv.at[chunk, hop - 1],
            device_id=(member, target),
            device_id_type=MESH,
        )

    def own_copy(chunk):
        return pltpu.make_async_copy(
            out_ref.at[owner, chunk], rows_ref.at[0, chunk, owner], own_sem.at[chunk]
        )

    def share(chunk, hop):
        target = ring_member((place + step * hop + members) % members)
        return pltpu.make_async_remote_copy(
            src_ref=rows_ref.at[0, chunk],
            dst_ref=rows_ref.at[hop, chunk],
            send_sem=b_send.at[chunk, hop - 1],
            recv_sem=b_recv.at[chunk, hop - 1],
            device_id=(target, owner),
            device_id_type=MESH,
        )

    sends_half = (place // half + side) % 2 == 0
    gets_half = (place // half + side) % 2 == 1

    for chunk in range(members):
        own_copy(chunk).start()
        for hop in range(1, owners):
            dispatch(chunk, hop).start()
    for chunk in range(members):
        own_copy(chunk).wait()
        for hop in range(1, owners):
            dispatch(chunk, hop).wait_recv()

        @pl.when(sends_half)
        def _(chunk=chunk):
            share(chunk, half).start()

        for hop in range(1, half):
            share(chunk, hop).start()
    for chunk in range(members):
        for hop in range(1, owners):
            dispatch(chunk, hop).wait_send()
        for hop in range(1, half):
            share(chunk, hop).wait()

        @pl.when(sends_half)
        def _(chunk=chunk):
            share(chunk, half).wait_send()

        @pl.when(gets_half)
        def _(chunk=chunk):
            share(chunk, half).wait_recv()


def exchange(outgoing, members, owners):
    sub, width = outgoing.shape[2:]
    slots = members // 2 + 1
    return pl.pallas_call(
        functools.partial(exchange_kernel, members, owners),
        out_shape=jax.ShapeDtypeStruct((slots, members, owners, sub, width), outgoing.dtype),
        in_specs=[pl.BlockSpec(memory_space=pltpu.VMEM)],
        out_specs=pl.BlockSpec(memory_space=pltpu.VMEM),
        scratch_shapes=[
            pltpu.SemaphoreType.DMA((members, owners - 1)),
            pltpu.SemaphoreType.DMA((members, owners - 1)),
            pltpu.SemaphoreType.DMA((members,)),
            pltpu.SemaphoreType.DMA((members, members // 2)),
            pltpu.SemaphoreType.DMA((members, members // 2)),
        ],
        compiler_params=pltpu.CompilerParams(
            collective_id=0, has_side_effects=True, vmem_limit_bytes=60 * 1024 * 1024
        ),
    )(outgoing)


def body(sketches, labels, places, counts, chosen):
    row_count, width = sketches.shape
    members = lax.axis_size("dp")
    owners = lax.axis_size("cls")
    devices = members * owners
    sub = 2 * row_count // devices
    capacity = devices * sub
    half = members // 2
    slots = half + 1
    member = lax.axis_index("dp")
    owner = lax.axis_index("cls")
    picked = chosen[:, 0]
    pick_count = picked.shape[0]

    target = (labels * members + places // capacity) * sub + places % sub
    send_table = (
        lax.broadcasted_iota(jnp.int32, (2 * row_count, row_count), 0) == target[None, :]
    ).astype(jnp.bfloat16)
    outgoing = jnp.dot(send_table, sketches, preferred_element_type=jnp.float32).astype(
        jnp.bfloat16
    )
    rows = exchange(outgoing.reshape(owners, members, sub, width), members, owners)
    rows = rows.reshape(slots * capacity, width)
    own = rows[:capacity]

    step = 1 - 2 * (owner % 2)
    place = ring_place(member)
    slot_member = jnp.stack(
        [ring_member((place - step * hop + members) % members) for hop in range(slots)]
    )
    has_half = (place // half + owner % 2) % 2 == 1
    slot_here = (jnp.arange(slots) < half) | has_half

    class_counts = counts[0]
    valid_places = (
        lax.broadcasted_iota(jnp.int32, (members, devices, sub), 2) < class_counts[:, :, None]
    )
    valid_blocks = jnp.transpose(
        valid_places.reshape(members, members, owners, sub), (1, 0, 2, 3)
    ).reshape(members, capacity)
    slot_valid = (
        jnp.stack([lax.dynamic_index_in_dim(valid_blocks, slot_member[s], 0, False) for s in range(slots)])
        & slot_here[:, None]
    )
    column_valid = slot_valid.reshape(-1)
    own_valid = slot_valid[0]
    total = jnp.sum(class_counts).astype(jnp.float32)

    source = picked % capacity // sub
    pick_index = (picked // capacity * owners + source % owners) * sub + picked % sub
    pick_table = (
        (jnp.arange(capacity)[None, :] == pick_index[:, None])
        & (source // owners == member)[:, None]
    ).astype(jnp.bfloat16)
    pick_part = jnp.dot(pick_table, own, preferred_element_type=jnp.float32).astype(jnp.bfloat16)
    pick_rows = jnp.sum(
        lax.all_gather(pick_part, "dp", axis=0).astype(jnp.float32), axis=0
    ).astype(jnp.bfloat16)

    wide = rows.astype(jnp.float32)
    norms = jnp.sum(wide * wide, axis=1)
    wide_picks = pick_rows.astype(jnp.float32)
    pick_norms = jnp.sum(wide_picks * wide_picks, axis=1)
    contract = (((1,), (1,)), ((), ()))
    inner = lax.dot_general(own, rows, contract, preferred_element_type=jnp.float32)
    pick_inner = lax.dot_general(pick_rows, rows, contract, preferred_element_type=jnp.float32)
    spread = (norms[:capacity, None] + norms[None, :] - 2.0 * inner) / width
    pick_spread = (pick_norms[:, None] + norms[None, :] - 2.0 * pick_inner) / width

    largest = jnp.max(
        jnp.where(own_valid[:, None] & column_valid[None, :], spread, 0.0)
    )
    bound = jnp.max(lax.all_gather(largest.reshape(1), "dp", axis=0))

    pick_similar = bound - pick_spread
    current = jnp.zeros((slots * capacity,), jnp.float32)
    column_gain = []
    row_gain = []
    similar = bound - spread
    far = similar[:, capacity:]
    for turn in range(pick_count):
        near_cover = current[:capacity]
        column_gain.append(
            jnp.sum(
                jnp.where(
                    own_valid[:, None] & column_valid[None, :],
                    jnp.maximum(similar - near_cover[:, None], 0.0),
                    0.0,
                ),
                axis=0,
            )
        )
        row_gain.append(
            jnp.sum(
                jnp.where(
                    column_valid[None, capacity:],
                    jnp.maximum(far - current[None, capacity:], 0.0),
                    0.0,
                ),
                axis=1,
            )
        )
        current = jnp.maximum(current, pick_similar[turn])
    column_gain = jnp.stack(column_gain).reshape(pick_count, slots, capacity)
    near_gain = column_gain[:, 0] + jnp.stack(row_gain)
    own_cover = current[:capacity]

    near = jnp.concatenate([near_gain, own_cover[None]], axis=0)
    held = jnp.concatenate(
        [
            near[:, None],
            jnp.concatenate(
                [column_gain[:, 1:], jnp.zeros((1, slots - 1, capacity), jnp.float32)], axis=0
            ),
        ],
        axis=1,
    )
    spots = jnp.arange(members)[:, None] == slot_member[None, :]
    spots = spots & slot_here[None, :]
    placed = jnp.sum(jnp.where(spots[None, :, :, None], held[:, None], 0.0), axis=2)
    placed = placed.reshape(pick_count + 1, members, members, owners, sub)
    placed = jnp.transpose(placed, (2, 0, 1, 3, 4)).reshape(members, pick_count + 1, capacity)
    summed = jnp.sum(
        lax.all_to_all(placed, "dp", split_axis=0, concat_axis=0, tiled=True), axis=0
    )
    place_valid = lax.dynamic_index_in_dim(
        valid_places.reshape(members, capacity), member, 0, keepdims=False
    ).astype(jnp.float32)
    gain_scores = (summed[:pick_count] * place_valid[None, :] / total)[:, None, :]
    coverage = (summed[pick_count] * place_valid)[None, :]
    return (gain_scores, coverage)


def solution(mesh):
    placed = (
        P(("dp", "cls"), None),
        P(("dp", "cls")),
        P(("dp", "cls")),
        P("cls", None, None),
        P(None, "cls"),
    )
    return jax.shard_map(
        body,
        mesh=mesh,
        in_specs=placed,
        out_specs=(P(None, "cls", "dp"), P("cls", "dp")),
        check_vma=False,
    )
```

time: 346 us -> 228 us (0.66)
  waiting for transfers between devices: 172 us -> 3.14 us
  Pallas kernels: 0 us -> 146 us
  blocking collectives: 108 us -> 18.5 us
  between operations: 20.5 us -> 1.78 us
  matrix products: 16.3 us -> 28 us
  other arithmetic: 21.9 us -> 16.5 us
  local copies, waits for them, and re-layouts: 5.43 us -> 9.8 us
    pallas_call x0 -> x1, Pallas kernels: none -> 146 us  [exchange(): pl.pallas_call(functools.partial(exchange_kernel, members, owners), out_s...]
    all_gather x1 -> x0, waiting for transfers between devices: 146 us -> none  [body(): block_rows = lax.all_gather(local_rows, 'dp', axis=0, tiled=True)]
    all_to_all x1 -> x0, blocking collectives: 98 us -> none  [body(): lax.all_to_all(outgoing.reshape(devices, per_source, width), ('dp', 'cls'...]
    unnamed x3 -> x0, waiting for transfers between devices: 26.2 us -> none
    unnamed x0 -> x1, blocking collectives: none -> 9.91 us
    dot_general x1 -> x3, matrix products: 15 us -> 24.8 us  [the longest x1 13.1 us: body(): lax.dot_general(own, rows, contract, preferred_element_type=jnp.float32)]
    pmax x1 -> x0, blocking collectives: 9.54 us -> none  [body(): bound = lax.pmax(largest, 'dp')]
    all_gather x0 -> x1, blocking collectives: none -> 8.58 us  [body(): lax.all_gather(pick_part, 'dp', axis=0).astype(jnp.float32)]
  transfers between devices with their start and end apart: 2 -> 1, of which waited for: 2 -> 1; matrix products, arithmetic and copies ran while one was open for 2% -> 0% of each run, Pallas kernels for 0% -> 0%
where the time goes in v1:
time: 228 us; the launch traced here: 227 us
  Pallas kernels  146 us (64%)
  matrix products  28 us (12%)
  blocking collectives  18.5 us (8%)
  other arithmetic  16.5 us (7%)
  local copies, waits for them, and re-layouts  9.8 us (4%)
  starting transfers between devices  3.26 us (1%)
  waiting for transfers between devices  3.14 us (1%)
    pallas_call x1, Pallas kernels, exchange(): pl.pallas_call(functools.partial(exchange_kernel, members, owners), out_s...  146 us
    dot_general x1, matrix products, body(): lax.dot_general(own, rows, contract, preferred_element_type=jnp.float32)  13.1 us
    unnamed x1, blocking collectives  9.91 us
    dot_general x1, matrix products, body(): lax.dot_general(pick_rows, rows, contract, preferred_element_type=jnp.flo...  8.81 us
    all_gather x1, blocking collectives, body(): lax.all_gather(pick_part, 'dp', axis=0).astype(jnp.float32)  8.58 us
    reduce_sum x1, other arithmetic, body(): norms = jnp.sum(wide * wide, axis=1)  7.05 us
    slice x1, local copies, waits for them, and re-layouts, body(): own = rows[:capacity]  4.68 us
  transfers between devices with their start and end apart: 1, of which 1 were waited for; matrix products, arithmetic and copies ran while one was open for 0% of the time, Pallas kernels for 0%

profile of v1, /device:TPU:8, one launch (start us, length us, event | category | flops | bytes accessed | tf_op | source)
XLA Modules:
  0.0 227.4 jit_solution(6442431817917205866)
XLA Ops:
  0.9 0.9 lt.139
  2.3 0.7 fusion.18
  3.0 3.2 %convolution_convert_fusion = bf16[512,4096]{1,0:T(8,128)(2,1)} fusion(bf16[256,4096]{1,0:T(8,128)(2,1)S(1)} %copy-done, s32[256]{0:T(256)S(1)} %fusion.18), kind=kOutput, calls=%fused_computation.1 | convolution fusion | flops 1075970048 | bytes 6292480 | tf_op jit(solution)/shard_map/dot_general | solution.py:144
  6.2 146.4 %shard_map.68 = bf16[3,4,8,16,4096]{4,3,2,1,0:T(8,128)(2,1)} custom-call(bf16[8,4,16,4096]{3,2,1,0:T(8,128)(2,1)} %bitcast.49), custom_call_target="tpu_custom_call" | custom-call | tf_op jit(solution)/shard_map/pallas_call | solution.py:108
  152.6 7.1 %multiply_reduce_fusion = f32[3,4,8,16]{3,2,1,0:T(8,128)S(1)} fusion(bf16[3,4,8,16,4096]{4,3,2,1,0:T(8,128)(2,1)} %shard_map.68), kind=kLoop, calls=%fused_computation | loop fusion | flops 18872832 | bytes 12589056 | tf_op jit(solution)/shard_map/reduce_sum | solution.py:186
  159.7 4.7 %slice.73 = bf16[1,4,8,16,4096]{4,3,2,1,0:T(8,128)(2,1)} slice(bf16[3,4,8,16,4096]{4,3,2,1,0:T(8,128)(2,1)} %shard_map.68), slice={[0:1], [0:4], [0:8], [0:16], [0:4096]} | slice | bytes 8388608 | tf_op jit(solution)/shard_map/slice | solution.py:149
  164.5 0.6 dynamic-slice
  165.1 13.1 %fusion.3 = (f32[]{:T(128)}, f32[512,1536]{1,0:T(8,128)}) fusion(pred[1536]{0:T(1024)(128)(4,1)S(1)} %and.222, pred[512]{0:T(512)(128)(4,1)S(1)} %slice_reduce_fusion, bf16[512,4096]{1,0:T(8,128)(2,1)} %bitcast.47, bf16[1536,4096]{1,0:T(8,128)(2,1)} %bitcast.45, f32[1536]{0:T(1024)S(1)} %add.210, f32[512]{0:T(512)S(1)} %add.208), kind=kOutput, calls=%fused_computation.11 | convolution fusion | flops 6447955968 | bytes 19933188 | tf_op jit(solution)/shard_map/dot_general | solution.py:190
  178.2 1.2 dynamic-update-slice
  179.5 9.9 %all-reduce.1 = f32[4]{0:T(128)S(1)} all-reduce(f32[4]{0:T(128)S(1)} %dynamic-update-slice), channel_id=1, replica_groups=mesh['dp'=4,'cls'=8] {'dp'}, use_global_device_ids=true, to_apply=%add.1 | all-reduce | flops 4 | bytes 32
  189.4 2.9 %fusion = bf16[1,3,4096]{2,1,0:T(4,128)(2,1)S(1)} fusion(bf16[512,4096]{1,0:T(8,128)(2,1)} %bitcast.48, s32[3]{0:T(128)S(1)} %fusion.21, pred[3]{0:T(512)(128)(4,1)S(1)} %get-tuple-element.17), kind=kOutput, calls=%fused_computation.7 | convolution fusion | flops 12598272 | bytes 4218895 | tf_op jit(solution)/shard_map/dot_general | solution.py:180
  192.3 8.6 %all-gather.1 = bf16[4,3,4096]{2,1,0:T(4,128)(2,1)S(1)} all-gather(bf16[1,3,4096]{2,1,0:T(4,128)(2,1)S(1)} %fusion), channel_id=2, replica_groups=mesh['dp'=4,'cls'=8] {'dp'}, dimensions={0}, use_global_device_ids=true | all-gather | bytes 122880 | tf_op jit(solution)/shard_map/all_gather | solution.py:182
  200.9 0.1 multiply_reduce_fusion.1
  201.1 0.6 reduce.3
  201.7 8.8 %fusion.9 = f32[3,1536]{1,0:T(4,128)S(1)} fusion(bf16[3,4096]{1,0:T(4,128)(2,1)S(1)} %reduce_sum.113, bf16[1536,4096]{1,0:T(8,128)(2,1)} %bitcast.46, f32[1536]{0:T(1024)S(1)} %add.210, f32[3]{0:T(128)S(1)} %multiply_reduce_fusion.1, f32[]{:T(128)} %reduce.3), kind=kOutput, calls=%fused_computation.18 | convolution fusion | flops 37771776 | bytes 12632080 | tf_op jit(solution)/shard_map/dot_general | solution.py:191
  210.6 3.7 %fusion.6 = (f32[1536]{0:T(1024)S(1)}, f32[1536]{0:T(1024)S(1)}, f32[1536]{0:T(1024)S(1)}, f32[512,1536]{1,0:T(8,128)}) fusion(f32[512]{0:T(512)S(1)} %bitcast.59, pred[1536]{0:T(1024)(128)(4,1)S(1)} %and.222, pred[512]{0:T(512)(128)(4,1)S(1)} %slice_reduce_fusion, f32[512]{0:T(512)S(1)} %bitcast.58, f32[512,1536]{1,0:T(8,128)S(1)} %copy-done.1, f32[]{:T(128)} %reduce.3), kind=kLoop, calls=%fused_computation.14 | loop fusion | flops 10219008 | bytes 6316036 | tf_op jit(solution)/shard_map/reduce_sum | solution.py:209
  214.6 2.5 %select_reduce_fusion.2 = (f32[512]{0:T(512)S(1)}, f32[512]{0:T(512)S(1)}, f32[512]{0:T(512)S(1)}) fusion(f32[512,1536]{1,0:T(8,128)} %get-tuple-element.16, pred[1024]{0:T(1024)(128)(4,1)S(1)} %broadcast_in_dim.84, f32[1024]{0:T(1024)S(1)} %bitcast.53, f32[1024]{0:T(1024)S(1)} %bitcast.54), kind=kLoop, calls=%fused_computation.21 | loop fusion | flops 5765632 | bytes 2112512 | tf_op jit(solution)/shard_map/reduce_sum | solution.py:219
  217.3 0.1 reshape.124
  217.5 0.8 reshape.125
  218.2 3.3 %all-to-all-start = ((f32[4,4,512]{2,1,0:T(4,128)}), f32[4,4,512]{2,1,0:T(4,128)S(1)}, u32[]{:S(2)}, u32[]{:S(2)}) async-start(f32[4,4,512]{2,1,0:T(4,128)} %reshape.125), calls=%async_computation | async-start | bytes 65536 | tf_op jit(solution)/shard_map/all_to_all | solution.py:249
  221.8 0.6 reduce_sum.122
  223.1 3.1 %all-to-all-done = f32[4,4,512]{2,1,0:T(4,128)S(1)} async-done(((f32[4,4,512]{2,1,0:T(4,128)}), f32[4,4,512]{2,1,0:T(4,128)S(1)}, u32[]{:S(2)}, u32[]{:S(2)}) %all-to-all-start) | async-done | bytes 32800 | tf_op jit(solution)/shard_map/all_to_all | solution.py:249
  226.2 0.6 compare_select_fusion
  226.8 0.6 copy.23
  (58 shorter events, 1.5 us)
Async XLA Ops:
  0.6 2.3 %copy-start = (bf16[256,4096]{1,0:T(8,128)(2,1)S(1)}, bf16[256,4096]{1,0:T(8,128)(2,1)}, u32[]{:S(2)}) copy-start(bf16[256,4096]{1,0:T(8,128)(2,1)} %param.5) | copy-start | bytes 6291460
  159.7 4.8 %copy-start.4 = (u32[32]{0:T(128)S(1)}, u32[32]{0:T(128)}, u32[]{:S(2)}) copy-start(u32[32]{0:T(128)} %constant.240) | copy-start | bytes 388
  165.1 24.3 %copy-start.3 = (s32[3,1]{0,1:T(1,128)S(1)}, s32[3,1]{0,1:T(1,128)}, u32[]{:S(2)}) copy-start(s32[3,1]{0,1:T(1,128)} %param.9) | copy-start | bytes 40
  201.7 8.9 %copy-start.1 = (f32[512,1536]{1,0:T(8,128)S(1)}, f32[512,1536]{1,0:T(8,128)}, u32[]{:S(2)}) copy-start(f32[512,1536]{1,0:T(8,128)} %get-tuple-element.28) | copy-start | bytes 9437188
  214.4 7.1 %copy-start.2 = (s32[1,4,32]{2,1,0:T(4,128)S(1)}, s32[1,4,32]{2,1,0:T(4,128)}, u32[]{:S(2)}) copy-start(s32[1,4,32]{2,1,0:T(4,128)} %param.8) | copy-start | bytes 1540
  218.2 8.0 %all-to-all-start = ((f32[4,4,512]{2,1,0:T(4,128)}), f32[4,4,512]{2,1,0:T(4,128)S(1)}, u32[]{:S(2)}, u32[]{:S(2)}) async-start(f32[4,4,512]{2,1,0:T(4,128)} %reshape.125), calls=%async_computation | async-start | bytes 65536 | tf_op jit(solution)/shard_map/all_to_all | solution.py:249

commit v2 on v1

--- a/solution.py
+++ b/solution.py
@@ -20,13 +20,36 @@
     return 2 * high + (place % 2 + high) % 2
 
 
-def exchange_kernel(members, owners, out_ref, rows_ref, a_send, a_recv, own_sem, b_send, b_recv):
+def exchange_kernel(
+    members,
+    owners,
+    out_ref,
+    table_ref,
+    inner_ref,
+    pick_inner_ref,
+    norms_ref,
+    pick_norms_ref,
+    rows_ref,
+    picks_ref,
+    a_send,
+    a_recv,
+    own_sem,
+    b_send,
+    b_recv,
+    p_send,
+    p_recv,
+):
     member = lax.axis_index("dp")
     owner = lax.axis_index("cls")
+    chunks, unit, width = out_ref.shape[1:]
+    capacity = chunks * owners * unit
+    group = min(chunks, max(1, 256 // (owners * unit)))
+    span = group * owners * unit
     half = members // 2
     place = ring_place(member)
     side = owner % 2
     step = 1 - 2 * side
+    contract = (((1,), (1,)), ((), ()))
 
     barrier = pltpu.get_barrier_semaphore()
     for hop in range(1, owners):
@@ -42,11 +65,13 @@
         )
     pl.semaphore_wait(barrier, owners + members - 2)
 
+    mine = pl.ds(pl.multiple_of(owner * unit, unit), unit)
+
     def dispatch(chunk, hop):
         target = (owner + hop) % owners
         return pltpu.make_async_remote_copy(
             src_ref=out_ref.at[target, chunk],
-            dst_ref=rows_ref.at[0, chunk, owner],
+            dst_ref=rows_ref.at[0, chunk, mine],
             send_sem=a_send.at[chunk, hop - 1],
             recv_sem=a_recv.at[chunk, hop - 1],
             device_id=(member, target),
@@ -55,7 +80,7 @@
 
     def own_copy(chunk):
         return pltpu.make_async_copy(
-            out_ref.at[owner, chunk], rows_ref.at[0, chunk, owner], own_sem.at[chunk]
+            out_ref.at[owner, chunk], rows_ref.at[0, chunk, mine], own_sem.at[chunk]
         )
 
     def share(chunk, hop):
@@ -69,14 +94,36 @@
             device_id_type=MESH,
         )
 
+    def share_picks(hop):
+        return pltpu.make_async_remote_copy(
+            src_ref=picks_ref.at[0],
+            dst_ref=picks_ref.at[hop],
+            send_sem=p_send.at[hop - 1],
+            recv_sem=p_recv.at[hop - 1],
+            device_id=(ring_member((place + hop) % members), owner),
+            device_id_type=MESH,
+        )
+
+    def own_rows():
+        return rows_ref[0].reshape(capacity, width)
+
+    def multiply(slot, first):
+        block = rows_ref[slot, first : first + group].reshape(span, width)
+        low = slot * capacity + first * owners * unit
+        inner_ref[:, low : low + span] = lax.dot_general(
+            own_rows(), block, contract, preferred_element_type=jnp.float32
+        )
+        wide = block.astype(jnp.float32)
+        norms_ref[low : low + span, :] = jnp.sum(wide * wide, axis=1, keepdims=True)
+
     sends_half = (place // half + side) % 2 == 0
     gets_half = (place // half + side) % 2 == 1
 
-    for chunk in range(members):
+    for chunk in range(chunks):
         own_copy(chunk).start()
         for hop in range(1, owners):
             dispatch(chunk, hop).start()
-    for chunk in range(members):
+    for chunk in range(chunks):
         own_copy(chunk).wait()
         for hop in range(1, owners):
             dispatch(chunk, hop).wait_recv()
@@ -87,40 +134,98 @@
 
         for hop in range(1, half):
             share(chunk, hop).start()
-    for chunk in range(members):
+
+    picks_ref[0] = lax.dot_general(
+        table_ref[...],
+        own_rows(),
+        (((1,), (0,)), ((), ())),
+        preferred_element_type=jnp.float32,
+    ).astype(picks_ref.dtype)
+    for first in range(0, chunks, group):
+        multiply(0, first)
+    for hop in range(1, members):
+        share_picks(hop).start()
+
+    for first in range(0, chunks, group):
+        for hop in range(1, half):
+            for chunk in range(first, first + group):
+                share(chunk, hop).wait_recv()
+            multiply(hop, first)
+
+        @pl.when(gets_half)
+        def _(first=first):
+            for chunk in range(first, first + group):
+                share(chunk, half).wait_recv()
+            multiply(half, first)
+
+    for hop in range(1, members):
+        share_picks(hop).wait_recv()
+    picks = picks_ref[0].astype(jnp.float32)
+    for hop in range(1, members):
+        picks = picks + picks_ref[hop].astype(jnp.float32)
+    pick_norms_ref[...] = jnp.sum(picks * picks, axis=1, keepdims=True)
+    picks = picks.astype(picks_ref.dtype)
+
+    def multiply_picks(slot):
+        pick_inner_ref[:, slot * capacity : (slot + 1) * capacity] = lax.dot_general(
+            picks,
+            rows_ref[slot].reshape(capacity, width),
+            contract,
+            preferred_element_type=jnp.float32,
+        )
+
+    for slot in range(half):
+        multiply_picks(slot)
+
+    @pl.when(gets_half)
+    def _():
+        multiply_picks(half)
+
+    for chunk in range(chunks):
         for hop in range(1, owners):
             dispatch(chunk, hop).wait_send()
         for hop in range(1, half):
-            share(chunk, hop).wait()
+            share(chunk, hop).wait_send()
 
         @pl.when(sends_half)
         def _(chunk=chunk):
             share(chunk, half).wait_send()
 
-        @pl.when(gets_half)
-        def _(chunk=chunk):
-            share(chunk, half).wait_recv()
-
-
-def exchange(outgoing, members, owners):
-    sub, width = outgoing.shape[2:]
+    for hop in range(1, members):
+        share_picks(hop).wait_send()
+
+
+def exchange(outgoing, pick_table, members, owners):
+    chunks, unit, width = outgoing.shape[1:]
+    capacity = chunks * owners * unit
+    padded = pick_table.shape[0]
     slots = members // 2 + 1
+    vmem = pl.BlockSpec(memory_space=pltpu.VMEM)
     return pl.pallas_call(
         functools.partial(exchange_kernel, members, owners),
-        out_shape=jax.ShapeDtypeStruct((slots, members, owners, sub, width), outgoing.dtype),
-        in_specs=[pl.BlockSpec(memory_space=pltpu.VMEM)],
-        out_specs=pl.BlockSpec(memory_space=pltpu.VMEM),
+        out_shape=(
+            jax.ShapeDtypeStruct((capacity, slots * capacity), jnp.float32),
+            jax.ShapeDtypeStruct((padded, slots * capacity), jnp.float32),
+            jax.ShapeDtypeStruct((slots * capacity, 1), jnp.float32),
+            jax.ShapeDtypeStruct((padded, 1), jnp.float32),
+        ),
+        in_specs=[vmem, vmem],
+        out_specs=(vmem, vmem, vmem, vmem),
         scratch_shapes=[
-            pltpu.SemaphoreType.DMA((members, owners - 1)),
-            pltpu.SemaphoreType.DMA((members, owners - 1)),
-            pltpu.SemaphoreType.DMA((members,)),
-            pltpu.SemaphoreType.DMA((members, members // 2)),
-            pltpu.SemaphoreType.DMA((members, members // 2)),
+            pltpu.VMEM((slots, chunks, owners * unit, width), outgoing.dtype),
+            pltpu.VMEM((members, padded, width), outgoing.dtype),
+            pltpu.SemaphoreType.DMA((chunks, owners - 1)),
+            pltpu.SemaphoreType.DMA((chunks, owners - 1)),
+            pltpu.SemaphoreType.DMA((chunks,)),
+            pltpu.SemaphoreType.DMA((chunks, members // 2)),
+            pltpu.SemaphoreType.DMA((chunks, members // 2)),
+            pltpu.SemaphoreType.DMA((members - 1,)),
+            pltpu.SemaphoreType.DMA((members - 1,)),
         ],
         compiler_params=pltpu.CompilerParams(
             collective_id=0, has_side_effects=True, vmem_limit_bytes=60 * 1024 * 1024
         ),
-    )(outgoing)
+    )(outgoing, pick_table)
 
 
 def body(sketches, labels, places, counts, chosen):
@@ -130,6 +235,8 @@
     devices = members * owners
     sub = 2 * row_count // devices
     capacity = devices * sub
+    unit = 16
+    chunks = members * sub // unit
     half = members // 2
     slots = half + 1
     member = lax.axis_index("dp")
@@ -144,10 +251,6 @@
     outgoing = jnp.dot(send_table, sketches, preferred_element_type=jnp.float32).astype(
         jnp.bfloat16
     )
-    rows = exchange(outgoing.reshape(owners, members, sub, width), members, owners)
-    rows = rows.reshape(slots * capacity, width)
-    own = rows[:capacity]
-
     step = 1 - 2 * (owner % 2)
     place = ring_place(member)
     slot_member = jnp.stack(
@@ -161,7 +264,10 @@
         lax.broadcasted_iota(jnp.int32, (members, devices, sub), 2) < class_counts[:, :, None]
     )
     valid_blocks = jnp.transpose(
-        valid_places.reshape(members, members, owners, sub), (1, 0, 2, 3)
+        jnp.transpose(valid_places.reshape(members, members, owners, sub), (1, 2, 0, 3)).reshape(
+            members, owners, chunks, unit
+        ),
+        (0, 2, 1, 3),
     ).reshape(members, capacity)
     slot_valid = (
         jnp.stack([lax.dynamic_index_in_dim(valid_blocks, slot_member[s], 0, False) for s in range(slots)])
@@ -172,25 +278,22 @@
     total = jnp.sum(class_counts).astype(jnp.float32)
 
     source = picked % capacity // sub
-    pick_index = (picked // capacity * owners + source % owners) * sub + picked % sub
+    offset = picked // capacity * sub + picked % sub
+    pick_index = (offset // unit * owners + source % owners) * unit + offset % unit
     pick_table = (
         (jnp.arange(capacity)[None, :] == pick_index[:, None])
         & (source // owners == member)[:, None]
     ).astype(jnp.bfloat16)
-    pick_part = jnp.dot(pick_table, own, preferred_element_type=jnp.float32).astype(jnp.bfloat16)
-    pick_rows = jnp.sum(
-        lax.all_gather(pick_part, "dp", axis=0).astype(jnp.float32), axis=0
-    ).astype(jnp.bfloat16)
-
-    wide = rows.astype(jnp.float32)
-    norms = jnp.sum(wide * wide, axis=1)
-    wide_picks = pick_rows.astype(jnp.float32)
-    pick_norms = jnp.sum(wide_picks * wide_picks, axis=1)
-    contract = (((1,), (1,)), ((), ()))
-    inner = lax.dot_general(own, rows, contract, preferred_element_type=jnp.float32)
-    pick_inner = lax.dot_general(pick_rows, rows, contract, preferred_element_type=jnp.float32)
+    pick_table = jnp.pad(pick_table, ((0, -pick_count % 16), (0, 0)))
+
+    inner, pick_inner, norms, pick_norms = exchange(
+        outgoing.reshape(owners, chunks, unit, width), pick_table, members, owners
+    )
+    norms = norms[:, 0]
     spread = (norms[:capacity, None] + norms[None, :] - 2.0 * inner) / width
-    pick_spread = (pick_norms[:, None] + norms[None, :] - 2.0 * pick_inner) / width
+    pick_spread = (
+        pick_norms[:pick_count] + norms[None, :] - 2.0 * pick_inner[:pick_count]
+    ) / width
 
     largest = jnp.max(
         jnp.where(own_valid[:, None] & column_valid[None, :], spread, 0.0)
@@ -243,8 +346,10 @@
     spots = jnp.arange(members)[:, None] == slot_member[None, :]
     spots = spots & slot_here[None, :]
     placed = jnp.sum(jnp.where(spots[None, :, :, None], held[:, None], 0.0), axis=2)
-    placed = placed.reshape(pick_count + 1, members, members, owners, sub)
-    placed = jnp.transpose(placed, (2, 0, 1, 3, 4)).reshape(members, pick_count + 1, capacity)
+    placed = jnp.transpose(
+        placed.reshape(pick_count + 1, members, chunks, owners, unit), (0, 1, 3, 2, 4)
+    ).reshape(pick_count + 1, members, owners, members, sub)
+    placed = jnp.transpose(placed, (3, 0, 1, 2, 4)).reshape(members, pick_count + 1, capacity)
     summed = jnp.sum(
         lax.all_to_all(placed, "dp", split_axis=0, concat_axis=0, tiled=True), axis=0
     )

time: 228 us -> 202 us (0.89)
  matrix products: 28 us -> 3.19 us
  blocking collectives: 18.5 us -> 12.5 us
  Pallas kernels: 146 us -> 151 us
  local copies, waits for them, and re-layouts: 9.8 us -> 6.81 us
  other arithmetic: 16.5 us -> 19.1 us
    dot_general x3 -> x0, matrix products: 24.8 us -> none  [the longest x1 13.1 us: body(): lax.dot_general(own, rows, contract, preferred_element_type=jnp.float32)]
    all_gather x1 -> x0, blocking collectives: 8.58 us -> none  [body(): lax.all_gather(pick_part, 'dp', axis=0).astype(jnp.float32)]
    reduce_sum x3 -> x0, other arithmetic: 7.27 us -> none  [the longest x1 7.05 us: body(): norms = jnp.sum(wide * wide, axis=1)]
    pallas_call x1, Pallas kernels: 146 us -> 151 us  [exchange(): pl.pallas_call(functools.partial(exchange_kernel, members, owners), out_s...]
    slice x1, local copies, waits for them, and re-layouts: 4.68 us -> 0.79 us  [body(): pick_norms[:pick_count] + norms[None, :] - 2.0 * pick_inner[:pick_count]]
    reduce_max x0 -> x1, other arithmetic: none -> 3.41 us  [body(): jnp.max(jnp.where(own_valid[:, None] & column_valid[None, :], spread, 0.0))]
    unnamed x1, blocking collectives: 9.91 us -> 12.5 us
where the time goes in v2:
time: 202 us; the launch traced here: 201 us
  Pallas kernels  151 us (75%)
  other arithmetic  19.1 us (9%)
  blocking collectives  12.5 us (6%)
  local copies, waits for them, and re-layouts  6.81 us (3%)
  starting transfers between devices  3.26 us (2%)
  matrix products  3.19 us (2%)
  waiting for transfers between devices  3.14 us (2%)
    pallas_call x1, Pallas kernels, exchange(): pl.pallas_call(functools.partial(exchange_kernel, members, owners), out_s...  151 us
    unnamed x1, blocking collectives  12.5 us
    reduce_sum x1, other arithmetic, body(): jnp.sum(jnp.where(own_valid[:, None] & column_valid[None, :], jnp.maximum...  5.32 us
  transfers between devices with their start and end apart: 1, of which 1 were waited for; matrix products, arithmetic and copies ran while one was open for 0% of the time, Pallas kernels for 0%

profile of v2, /device:TPU:8, one launch (start us, length us, event | category | flops | bytes accessed | tf_op | source)
XLA Modules:
  0.0 201.1 jit_solution(4345389142409407535)
XLA Ops:
  0.9 0.9 lt.143
  2.3 0.7 compare_bitcast_fusion
  3.0 0.7 fusion.14
  3.7 0.6 pad_convert_fusion.table_ref
  4.3 0.7 fusion.10
  5.0 3.2 %convolution_convert_fusion = bf16[512,4096]{1,0:T(8,128)(2,1)} fusion(bf16[256,4096]{1,0:T(8,128)(2,1)S(1)} %copy-done, s32[256]{0:T(256)S(1)} %fusion.10), kind=kOutput, calls=%fused_computation | convolution fusion | flops 1075970048 | bytes 6292480 | tf_op jit(solution)/shard_map/dot_general | solution.py:251
  8.2 151.3 %shard_map.68 = (f32[512,1536]{1,0:T(8,128)}, f32[16,1536]{1,0:T(8,128)}, f32[1536,1]{1,0:T(8,128)}, f32[16,1]{1,0:T(8,128)}) custom-call(bf16[8,4,16,4096]{3,2,1,0:T(8,128)(2,1)} %bitcast.32, bf16[16,512]{1,0:T(8,128)(2,1)} %pad_convert_fusion.table_ref), custom_call_target="tpu_custom_call" | custom-call | tf_op jit(solution)/shard_map/pallas_call | solution.py:204
  159.6 1.1 slice_reduce_fusion
  160.7 1.4 reduce.5
  162.1 0.8 slice_reduce_fusion.2
  162.9 0.6 dynamic-slice
  163.4 3.4 %fusion = f32[]{:T(128)} fusion(f32[512,1536]{1,0:T(8,128)} %get-tuple-element.7, f32[1536]{0:T(1024)S(1)} %reduce.5, f32[512]{0:T(512)S(1)} %slice_reduce_fusion, pred[1536]{0:T(1024)(128)(4,1)S(1)} %and.233, pred[512]{0:T(512)(128)(4,1)S(1)} %slice_reduce_fusion.1), kind=kLoop, calls=%fused_computation.5 | loop fusion | flops 5505023 | bytes 3155972 | tf_op jit(solution)/shard_map/reduce_max | solution.py:298
  166.9 1.2 dynamic-update-slice
  168.1 12.5 %all-reduce.2 = f32[4]{0:T(128)S(1)} all-reduce(f32[4]{0:T(128)S(1)} %dynamic-update-slice), channel_id=1, replica_groups=mesh['dp'=4,'cls'=8] {'dp'}, use_global_device_ids=true, to_apply=%add.2 | all-reduce | flops 4 | bytes 32
  180.6 0.6 reduce.1
  181.2 1.4 multiply_subtract_fusion
  182.7 5.3 %fusion.3 = (f32[1536]{0:T(1024)S(1)}, f32[1536]{0:T(1024)S(1)}, f32[1536]{0:T(1024)S(1)}, f32[512,1536]{1,0:T(8,128)}) fusion(f32[512]{0:T(512)S(1)} %bitcast.42, pred[1536]{0:T(1024)(128)(4,1)S(1)} %and.233, pred[512]{0:T(512)(128)(4,1)S(1)} %slice_reduce_fusion.1, f32[512]{0:T(512)S(1)} %bitcast.41, f32[512,1536]{1,0:T(8,128)} %get-tuple-element.7, ...), kind=kLoop, calls=%fused_computation.8 | loop fusion | flops 13364736 | bytes 6324228 | tf_op jit(solution)/shard_map/reduce_sum | solution.py:312
  188.2 2.5 %select_reduce_fusion.2 = (f32[512]{0:T(512)S(1)}, f32[512]{0:T(512)S(1)}, f32[512]{0:T(512)S(1)}) fusion(f32[512,1536]{1,0:T(8,128)} %get-tuple-element.22, pred[1024]{0:T(1024)(128)(4,1)S(1)} %broadcast_in_dim.81, f32[1024]{0:T(1024)S(1)} %bitcast.36, f32[1024]{0:T(1024)S(1)} %bitcast.37), kind=kLoop, calls=%fused_computation.13 | loop fusion | flops 5765632 | bytes 2112512 | tf_op jit(solution)/shard_map/reduce_sum | solution.py:322
  191.1 0.8 reshape.116
  191.9 3.3 %all-to-all-start = ((f32[4,4,512]{2,1,0:T(4,128)}), f32[4,4,512]{2,1,0:T(4,128)S(1)}, u32[]{:S(2)}, u32[]{:S(2)}) async-start(f32[4,4,512]{2,1,0:T(4,128)} %reshape.116), calls=%async_computation | async-start | bytes 65536 | tf_op jit(solution)/shard_map/all_to_all | solution.py:354
  195.5 0.6 reduce_sum.89
  196.7 3.1 %all-to-all-done = f32[4,4,512]{2,1,0:T(4,128)S(1)} async-done(((f32[4,4,512]{2,1,0:T(4,128)}), f32[4,4,512]{2,1,0:T(4,128)S(1)}, u32[]{:S(2)}, u32[]{:S(2)}) %all-to-all-start) | async-done | bytes 32800 | tf_op jit(solution)/shard_map/all_to_all | solution.py:354
  199.9 0.6 compare_select_fusion
  200.5 0.6 copy.19
  (50 shorter events, 1.4 us)
Async XLA Ops:
  0.6 4.4 %copy-start = (bf16[256,4096]{1,0:T(8,128)(2,1)S(1)}, bf16[256,4096]{1,0:T(8,128)(2,1)}, u32[]{:S(2)}) copy-start(bf16[256,4096]{1,0:T(8,128)(2,1)} %param.5) | copy-start | bytes 6291460
  8.2 154.6 %copy-start.2 = (u32[32]{0:T(128)S(1)}, u32[32]{0:T(128)}, u32[]{:S(2)}) copy-start(u32[32]{0:T(128)} %constant.255) | copy-start | bytes 388
  188.0 7.2 %copy-start.1 = (s32[1,4,32]{2,1,0:T(4,128)S(1)}, s32[1,4,32]{2,1,0:T(4,128)}, u32[]{:S(2)}) copy-start(s32[1,4,32]{2,1,0:T(4,128)} %param.8) | copy-start | bytes 1540
  191.9 8.0 %all-to-all-start = ((f32[4,4,512]{2,1,0:T(4,128)}), f32[4,4,512]{2,1,0:T(4,128)S(1)}, u32[]{:S(2)}, u32[]{:S(2)}) async-start(f32[4,4,512]{2,1,0:T(4,128)} %reshape.116), calls=%async_computation | async-start | bytes 65536 | tf_op jit(solution)/shard_map/all_to_all | solution.py:354

commit v3 on v2

--- a/solution.py
+++ b/solution.py
@@ -298,7 +298,11 @@
     largest = jnp.max(
         jnp.where(own_valid[:, None] & column_valid[None, :], spread, 0.0)
     )
-    bound = jnp.max(lax.all_gather(largest.reshape(1), "dp", axis=0))
+    bound = jnp.max(
+        lax.all_to_all(
+            jnp.broadcast_to(largest, (members, 1, 128)), "dp", split_axis=0, concat_axis=0, tiled=True
+        )
+    )
 
     pick_similar = bound - pick_spread
     current = jnp.zeros((slots * capacity,), jnp.float32)

time: 202 us -> 199 us (0.985)
  blocking collectives: 12.5 us -> 0 us
  starting transfers between devices: 3.26 us -> 9.58 us
  waiting for transfers between devices: 3.14 us -> 6.77 us
    unnamed x1 -> x0, blocking collectives: 12.5 us -> none
    all_to_all x0 -> x1, starting transfers between devices: none -> 6.32 us  [body(): lax.all_to_all(jnp.broadcast_to(largest, (members, 1, 128)), 'dp', split_...]
    all_to_all x0 -> x1, waiting for transfers between devices: none -> 3.35 us  [body(): lax.all_to_all(jnp.broadcast_to(largest, (members, 1, 128)), 'dp', split_...]
  transfers between devices with their start and end apart: 1 -> 2, of which waited for: 1 -> 2; matrix products, arithmetic and copies ran while one was open for 0% -> 1% of each run, Pallas kernels for 0% -> 0%
where the time goes in v3:
time: 199 us; the launch traced here: 198 us
  Pallas kernels  151 us (76%)
  other arithmetic  19.3 us (10%)
  starting transfers between devices  9.58 us (5%)
  waiting for transfers between devices  6.77 us (3%)
  local copies, waits for them, and re-layouts  6.17 us (3%)
  matrix products  3.18 us (2%)
    pallas_call x1, Pallas kernels, exchange(): pl.pallas_call(functools.partial(exchange_kernel, members, owners), out_s...  151 us
    all_to_all x1, starting transfers between devices, body(): lax.all_to_all(jnp.broadcast_to(largest, (members, 1, 128)), 'dp', split_...  6.32 us
    reduce_sum x1, other arithmetic, body(): jnp.sum(jnp.where(own_valid[:, None] & column_valid[None, :], jnp.maximum...  5.4 us
  transfers between devices with their start and end apart: 2, of which 2 were waited for; matrix products, arithmetic and copies ran while one was open for 1% of the time, Pallas kernels for 0%

profile of v3, /device:TPU:8, one launch (start us, length us, event | category | flops | bytes accessed | tf_op | source)
XLA Modules:
  0.0 198.0 jit_solution(2393860486764117409)
XLA Ops:
  0.9 0.9 lt.143
  2.3 0.7 compare_bitcast_fusion
  2.9 0.7 fusion.14
  3.7 0.6 pad_convert_fusion.table_ref
  4.3 0.7 fusion.10
  5.0 3.2 %convolution_convert_fusion = bf16[512,4096]{1,0:T(8,128)(2,1)} fusion(bf16[256,4096]{1,0:T(8,128)(2,1)S(1)} %copy-done, s32[256]{0:T(256)S(1)} %fusion.10), kind=kOutput, calls=%fused_computation | convolution fusion | flops 1075970048 | bytes 6292480 | tf_op jit(solution)/shard_map/dot_general | solution.py:251
  8.2 151.3 %shard_map.68 = (f32[512,1536]{1,0:T(8,128)}, f32[16,1536]{1,0:T(8,128)}, f32[1536,1]{1,0:T(8,128)}, f32[16,1]{1,0:T(8,128)}) custom-call(bf16[8,4,16,4096]{3,2,1,0:T(8,128)(2,1)} %bitcast.31, bf16[16,512]{1,0:T(8,128)(2,1)} %pad_convert_fusion.table_ref), custom_call_target="tpu_custom_call" | custom-call | tf_op jit(solution)/shard_map/pallas_call | solution.py:204
  159.5 1.1 slice_reduce_fusion
  160.6 1.4 reduce.3
  162.1 3.4 %fusion = f32[]{:T(128)} fusion(f32[512,1536]{1,0:T(8,128)} %get-tuple-element.7, f32[1536]{0:T(1024)S(1)} %reduce.3, f32[512]{0:T(512)S(1)} %slice_reduce_fusion, pred[1536]{0:T(1024)(128)(4,1)S(1)} %and.233, pred[512]{0:T(512)(128)(4,1)S(1)} %slice_reduce_fusion.1), kind=kLoop, calls=%fused_computation.5 | loop fusion | flops 5505023 | bytes 3155972 | tf_op jit(solution)/shard_map/reduce_max | solution.py:298
  165.5 1.1 broadcast_in_dim.83
  166.6 6.3 %all-to-all-start = ((f32[4,1,128]{2,1,0:T(1,128)}), f32[4,1,128]{2,1,0:T(1,128)S(1)}, u32[]{:S(2)}, u32[]{:S(2)}) async-start(f32[4,1,128]{2,1,0:T(1,128)} %broadcast_in_dim.83), calls=%async_computation | async-start | bytes 4096 | tf_op jit(solution)/shard_map/all_to_all | solution.py:302
  173.1 0.8 slice_reduce_fusion.2
  174.2 3.4 %all-to-all-done = f32[4,1,128]{2,1,0:T(1,128)S(1)} async-done(((f32[4,1,128]{2,1,0:T(1,128)}), f32[4,1,128]{2,1,0:T(1,128)S(1)}, u32[]{:S(2)}, u32[]{:S(2)}) %all-to-all-start) | async-done | bytes 2080 | tf_op jit(solution)/shard_map/all_to_all | solution.py:302
  177.6 0.6 reduce_max.19
  178.2 1.5 multiply_subtract_fusion
  179.7 5.4 %fusion.3 = (f32[1536]{0:T(1024)S(1)}, f32[1536]{0:T(1024)S(1)}, f32[1536]{0:T(1024)S(1)}, f32[512,1536]{1,0:T(8,128)}) fusion(f32[512]{0:T(512)S(1)} %bitcast.41, pred[1536]{0:T(1024)(128)(4,1)S(1)} %and.233, pred[512]{0:T(512)(128)(4,1)S(1)} %slice_reduce_fusion.1, f32[512]{0:T(512)S(1)} %bitcast.40, f32[512,1536]{1,0:T(8,128)} %get-tuple-element.7, ...), kind=kLoop, calls=%fused_computation.8 | loop fusion | flops 13364736 | bytes 6324228 | tf_op jit(solution)/shard_map/reduce_sum | solution.py:316
  185.2 2.5 %select_reduce_fusion.2 = (f32[512]{0:T(512)S(1)}, f32[512]{0:T(512)S(1)}, f32[512]{0:T(512)S(1)}) fusion(f32[512,1536]{1,0:T(8,128)} %get-tuple-element.24, pred[1024]{0:T(1024)(128)(4,1)S(1)} %broadcast_in_dim.85, f32[1024]{0:T(1024)S(1)} %bitcast.35, f32[1024]{0:T(1024)S(1)} %bitcast.36), kind=kLoop, calls=%fused_computation.13 | loop fusion | flops 5765632 | bytes 2112512 | tf_op jit(solution)/shard_map/reduce_sum | solution.py:326
  188.1 0.8 reshape.116
  188.8 3.3 %all-to-all-start.1 = ((f32[4,4,512]{2,1,0:T(4,128)}), f32[4,4,512]{2,1,0:T(4,128)S(1)}, u32[]{:S(2)}, u32[]{:S(2)}) async-start(f32[4,4,512]{2,1,0:T(4,128)} %reshape.116), calls=%async_computation.1 | async-start | bytes 65536 | tf_op jit(solution)/shard_map/all_to_all | solution.py:358
  192.1 0.6 reduce_sum.89
  193.4 3.4 %all-to-all-done.1 = f32[4,4,512]{2,1,0:T(4,128)S(1)} async-done(((f32[4,4,512]{2,1,0:T(4,128)}), f32[4,4,512]{2,1,0:T(4,128)S(1)}, u32[]{:S(2)}, u32[]{:S(2)}) %all-to-all-start.1) | async-done | bytes 32800 | tf_op jit(solution)/shard_map/all_to_all | solution.py:358
  196.8 0.6 compare_select_fusion
  197.4 0.6 copy.24
  (47 shorter events, 1.4 us)
Async XLA Ops:
  0.6 4.4 %copy-start = (bf16[256,4096]{1,0:T(8,128)(2,1)S(1)}, bf16[256,4096]{1,0:T(8,128)(2,1)}, u32[]{:S(2)}) copy-start(bf16[256,4096]{1,0:T(8,128)(2,1)} %param.5) | copy-start | bytes 6291460
  159.5 14.5 %copy-start.1 = (s32[1,4,32]{2,1,0:T(4,128)S(1)}, s32[1,4,32]{2,1,0:T(4,128)}, u32[]{:S(2)}) copy-start(s32[1,4,32]{2,1,0:T(4,128)} %param.8) | copy-start | bytes 1540
  166.6 10.9 %all-to-all-start = ((f32[4,1,128]{2,1,0:T(1,128)}), f32[4,1,128]{2,1,0:T(1,128)S(1)}, u32[]{:S(2)}, u32[]{:S(2)}) async-start(f32[4,1,128]{2,1,0:T(1,128)} %broadcast_in_dim.83), calls=%async_computation | async-start | bytes 4096 | tf_op jit(solution)/shard_map/all_to_all | solution.py:302
  188.8 8.0 %all-to-all-start.1 = ((f32[4,4,512]{2,1,0:T(4,128)}), f32[4,4,512]{2,1,0:T(4,128)S(1)}, u32[]{:S(2)}, u32[]{:S(2)}) async-start(f32[4,4,512]{2,1,0:T(4,128)} %reshape.116), calls=%async_computation.1 | async-start | bytes 65536 | tf_op jit(solution)/shard_map/all_to_all | solution.py:358
